TPU v7x, 32 devices: a whole 2x2x4 slice. The times are simulated.
32 devices in a mesh: pipe: 2 (over x), tensor: 2 (over core), dp: 8 (over z, y).
Axes of the slice: x: 2, y: 2, z: 4, core: 2. Of those that a mesh axis runs over, the one named last changes fastest.
Arguments:
- attn_out: bfloat16 [2, 4, 1024, 4096], P('pipe', None, 'dp', 'tensor'), may hold values from -6 to 6
- grad_top: bfloat16 [4, 1024, 4096], P(None, 'dp', 'tensor'), may hold values from -6 to 6
- branch_grad: bfloat16 [2, 4, 1024, 4096], P('pipe', None, 'dp', 'tensor'), may hold values from -6 to 6
- error_prev: bfloat16 [2, 8, 4096, 4096], P('pipe', 'dp', 'tensor'), may hold values from -0.3984375 to 0.3984375
- q_prev: float32 [2, 4096, 64], P('pipe', 'tensor'), may hold values from -6 to 6
Outputs:
- grad_input: bfloat16 [2, 4, 1024, 4096], P('pipe', None, 'dp', 'tensor')
- error_next: bfloat16 [2, 8, 4096, 4096], P('pipe', 'dp', 'tensor')
- p_factor: float32 [2, 4096, 64], P('pipe', 'tensor')
- q_factor: float32 [2, 4096, 64], P('pipe', 'tensor')
All inputs are finite; a program needn't handle non-finite values.
Results may differ from a plain program's by a relative error of at most 0.012.
Values may be sent and summed in bfloat16 or wider, within the bound.
A program may use at most 256 MiB of HBM per device.

v0:
```python
import functools

import jax
import jax.numpy as jnp
from jax import lax
from jax.experimental import pallas as pl
from jax.experimental.pallas import tpu as pltpu
from jax.sharding import PartitionSpec as P

BF16 = jnp.bfloat16
F32 = jnp.float32
NN = (((1,), (0,)), ((), ()))
NT = (((1,), (1,)), ((), ()))
TN = (((0,), (0,)), ((), ()))


def mm(a, b, dims):
    return lax.dot_general(a, b, dims, preferred_element_type=F32)


def terms(x):
    head = x.astype(BF16)
    tail = (x - head.astype(F32)).astype(BF16)
    return jnp.concatenate([head, tail], axis=0)


def fold(y):
    half = y.shape[0] // 2
    return y[:half] + y[half:]


def add_round(a, b):
    return (a.astype(F32) + b.astype(F32)).astype(BF16)


def inverse_factor(gram):
    rank = gram.shape[0]
    row = lax.broadcasted_iota(jnp.int32, (rank, 2 * rank), 0)
    col = lax.broadcasted_iota(jnp.int32, (rank, 2 * rank), 1)
    work = jnp.concatenate([gram, jnp.where(row == col, 1.0, 0.0)[:, :rank]], axis=1)
    for k in range(rank - 1):
        ratio = work[:, k : k + 1] * (1.0 / work[k : k + 1, k : k + 1])
        work = work - jnp.where(row > k, ratio * work[k : k + 1, :], 0.0)
    diagonal = jnp.sum(jnp.where(row == col, work, 0.0), axis=1, keepdims=True)
    return work[:, rank:] * lax.rsqrt(diagonal)


class Semaphores:
    def __init__(self):
        self.count = 0

    def take(self, n=1):
        first = self.count
        self.count += n
        return first


def semaphore_map(tensor, dp, units, tiles):
    s = Semaphores()
    names = {}
    for name, n in (
        ("err", tiles), ("load", 4),
        ("q_s", tensor), ("q_r", tensor), ("q0_s", 1), ("q0_r", 1),
        ("bulk_s", units), ("bulk_r", units), ("gx_s", 1), ("gx_r", 1),
        ("gq_s", tensor), ("gq_r", tensor), ("p_s", dp), ("p_r", dp),
        ("pg_s", dp), ("pg_r", dp), ("gram_s", tensor), ("gram_r", tensor),
        ("ap_s", tensor), ("ap_r", tensor), ("qx_s", tensor), ("qx_r", tensor),
        ("g_s", tensor * units), ("g_r", tensor * units), ("qp_s", dp), ("qp_r", dp),
        ("qg_s", dp), ("qg_r", dp), ("qf_s", tensor * dp), ("qf_r", tensor * dp),
    ):
        names[name] = s.take(n)
    return names, s.count


def chain_kernel(
    dims, attn_hbm, gtop_hbm, branch_hbm, err_hbm, q_hbm,
    matrix, grad_in, p_out, fact, pair, q_own,
    attn, gtop, branch, err, q_in, at_ref, qg, q0, gbuf, gqx, gqr, gqb, eq,
    psend, prcv, pg, praw, gb, lin, apb, apt, qx, qxr, qsend, qrcv, qf, sem,
):
    tensor, dp, units, tiles, names = dims
    tokens, head_rows = attn.shape
    features = gtop.shape[1]
    rank = q_in.shape[0]
    pw, qw = head_rows // dp, features // dp
    unit = features // units
    shards = unit // qw
    section = lax.axis_index("pipe")
    t = lax.axis_index("tensor")
    r = lax.axis_index("dp")
    scale = 1.0 / tokens

    def at(name, index=0):
        return sem.at[names[name] + index]

    def remote(src, dst, send, recv, **where):
        return pltpu.make_async_remote_copy(
            src_ref=src, dst_ref=dst, send_sem=send, recv_sem=recv,
            device_id=where, device_id_type=pl.DeviceIdType.MESH,
        )

    tensor_peers = [lax.rem(t + o, tensor) for o in range(1, tensor)]
    dp_peers = [lax.rem(r + o, dp) for o in range(1, dp)]

    def over_tensor(src, dst, key):
        return [
            remote(src, dst.at[t], at(key + "_s", o), at(key + "_r", t), tensor=peer)
            for o, peer in enumerate(tensor_peers)
        ]

    def from_tensor(dst, key):
        for peer in tensor_peers:
            remote(dst.at[peer], dst.at[peer], at(key + "_s"), at(key + "_r", peer), tensor=peer).wait_recv()

    def over_dp(src_of, dst, key):
        return [
            remote(src_of(peer), dst.at[r], at(key + "_s", o), at(key + "_r", r), dp=peer)
            for o, peer in enumerate(dp_peers)
        ]

    def from_dp(dst, key):
        for peer in dp_peers:
            remote(dst.at[peer], dst.at[peer], at(key + "_s"), at(key + "_r", peer), dp=peer).wait_recv()

    def start(copies):
        for copy in copies:
            copy.start()

    def sent(copies):
        for copy in copies:
            copy.wait_send()

    def columns(i):
        return pl.ds(pl.multiple_of(i * unit, unit), unit)

    tile = head_rows // tiles

    def err_copy(i):
        rows = pl.ds(pl.multiple_of(i * tile, tile), tile)
        return pltpu.make_async_copy(err_hbm.at[rows], err.at[rows], at("err", i))

    loads = [
        pltpu.make_async_copy(src, dst, at("load", i))
        for i, (src, dst) in enumerate(
            ((q_hbm, q_in), (branch_hbm, branch), (gtop_hbm, gtop), (attn_hbm, attn))
        )
    ]
    start(loads)
    for i in range(tiles):
        err_copy(i).start()

    barrier = pltpu.get_barrier_semaphore()
    for peer in tensor_peers:
        pl.semaphore_signal(barrier, inc=1, device_id={"tensor": peer}, device_id_type=pl.DeviceIdType.MESH)
    for peer in dp_peers:
        pl.semaphore_signal(barrier, inc=1, device_id={"dp": peer}, device_id_type=pl.DeviceIdType.MESH)
    pl.semaphore_signal(barrier, inc=1, device_id={"pipe": 1 - section}, device_id_type=pl.DeviceIdType.MESH)
    loads[0].wait()
    qg[t] = terms(q_in[...])
    loads[1].wait()
    pl.semaphore_wait(barrier, tensor + dp - 1)

    q0_copy = remote(qg.at[t, pl.ds(0, rank)], q0, at("q0_s"), at("q0_r"), pipe=1 - section)
    gx_copy = remote(gqx, gqr, at("gx_s"), at("gx_r"), pipe=1 - section)
    ahead = units // 4

    def bulk_copy(i):
        return remote(branch.at[:, columns(i)], gbuf.at[t, :, columns(i)], at("bulk_s", i), at("bulk_r", i), pipe=1 - section)

    @pl.when(section == 0)
    def _():
        q0_copy.start()

    @pl.when(section == 1)
    def _():
        for i in range(ahead):
            bulk_copy(i).start()

    q_copies = over_tensor(qg.at[t], qg, "q")
    start(q_copies)
    loads[2].wait()
    loads[3].wait()

    @pl.when(section == 1)
    def _():
        grad_in[...] = add_round(gtop[...], branch[...])
        gqb[t] = fold(mm(qg[t], gtop[...], NT)) * scale

    from_tensor(qg, "q")

    def eq_tile(i, carry):
        err_copy(i).wait()
        rows = pl.ds(pl.multiple_of(i * tile, tile), tile)
        total = mm(qg[0], err[rows, pl.ds(0, features)], NT)
        for tt in range(1, tensor):
            total += mm(qg[tt], err[rows, pl.ds(tt * features, features)], NT)
        eq[:, rows] = fold(total)
        return carry

    lax.fori_loop(0, tiles, eq_tile, 0)

    @pl.when(section == 1)
    def _():
        q0_copy.wait_recv()
        gqx[...] = (mm(q0[...], grad_in[...], NT) * scale).astype(BF16)
        gx_copy.start()
        for i in range(ahead, units):
            bulk_copy(i).start()

    @pl.when(section == 0)
    def _():
        gx_copy.wait_recv()
        gqb[t] = gqr[...].astype(F32)

    gq_copies = over_tensor(gqb.at[t], gqb, "gq")
    start(gq_copies)
    from_tensor(gqb, "gq")
    gq = gqb[0]
    for tt in range(1, tensor):
        gq += gqb[tt]
    p_local = (fold(mm(terms(gq), attn[...], NN)) + eq[:, :head_rows]).astype(BF16)
    for j in range(dp):
        psend[j] = p_local[:, j * pw : (j + 1) * pw]
    p_copies = over_dp(lambda peer: psend.at[peer], prcv, "p")
    start(p_copies)

    def g_copies(i):
        here = gbuf.at[t, :, columns(i)]
        return [
            remote(here, here, at("g_s", o * units + i), at("g_r", t * units + i), tensor=peer)
            for o, peer in enumerate(tensor_peers)
        ]

    def land_unit(i, carry):
        cols = columns(i)

        @pl.when(section == 0)
        def _():
            bulk_copy(i).wait_recv()
            out_grad = add_round(gtop[:, cols], gbuf[t, :, cols])
            gbuf[t, :, cols] = out_grad
            grad_in[:, cols] = add_round(out_grad, branch[:, cols])

        @pl.when(section == 1)
        def _():
            gbuf[t, :, cols] = gtop[:, cols]

        start(g_copies(i))
        return carry

    def matrix_unit(i, carry):
        cols = columns(i)
        for peer in tensor_peers:
            here = gbuf.at[peer, :, cols]
            remote(here, here, at("g_s"), at("g_r", peer * units + i), tensor=peer).wait_recv()
        block = min(head_rows, 512)
        for tt in range(tensor):
            there = pl.ds(pl.multiple_of(tt * features + i * unit, unit), unit)
            grads = gbuf[tt, :, cols]
            for c in range(head_rows // block):
                rows = pl.ds(c * block, block)
                value = mm(at_ref[rows, :], grads, NN) * scale + err[rows, there].astype(F32)
                matrix[rows, there] = value.astype(BF16)
        return carry

    def transpose_tile(i, carry):
        rows = pl.ds(pl.multiple_of(i * tile, tile), tile)
        at_ref[rows, :] = attn[:, rows].T
        return carry

    first, second, third = units // 4, 3 * units // 8, 5 * units // 8
    lax.fori_loop(0, tiles, transpose_tile, 0)
    lax.fori_loop(0, first, land_unit, 0)
    lax.fori_loop(0, first, matrix_unit, 0)
    from_dp(prcv, "p")
    total = psend[r].astype(F32)
    for peer in dp_peers:
        total += prcv[peer].astype(F32)
    pg[r] = (total * (1.0 / dp)).astype(BF16)
    pg_copies = over_dp(lambda peer: pg.at[r], pg, "pg")
    start(pg_copies)
    lax.fori_loop(first, second, land_unit, 0)
    lax.fori_loop(first, second, matrix_unit, 0)
    from_dp(pg, "pg")
    for j in range(dp):
        praw[:, j * pw : (j + 1) * pw] = pg[j]

    gb[t] = mm(praw[...], praw[...], NT)
    gram_copies = over_tensor(gb.at[t], gb, "gram")
    start(gram_copies)
    apb[t] = mm(praw[...], attn[...], NT) * scale
    ap_copies = over_tensor(apb.at[t], apb, "ap")
    start(ap_copies)

    step = min(features, 512)

    def project(owner, done):
        def column(i, carry):
            here = pl.ds(pl.multiple_of(i * step, step), step)
            there = pl.ds(pl.multiple_of(owner * features + i * step, step), step)
            done(here, mm(praw[...], err[:, there], NN))
            return carry

        lax.fori_loop(0, features // step, column, 0)

    qx_copies = []
    for o, peer in enumerate(tensor_peers):
        def keep(here, value, slot=o):
            qx[slot, :, here] = value.astype(BF16)

        project(peer, keep)
        copy = remote(qx.at[o], qxr.at[t], at("qx_s", o), at("qx_r", t), tensor=peer)
        copy.start()
        qx_copies.append(copy)

    def keep_own(here, value):
        eq[:, here] = value

    project(t, keep_own)
    lax.fori_loop(second, third, land_unit, 0)
    from_tensor(apb, "ap")
    ap = apb[0]
    for tt in range(1, tensor):
        ap += apb[tt]
    apt[...] = terms(ap)
    from_tensor(qxr, "qx")

    def q_copy(j):
        return remote(qsend.at[j], qrcv.at[r], at("qp_s", j), at("qp_r", r), dp=j)

    def q_unit(i, carry):
        cols = columns(i)
        value = eq[:, cols] + fold(mm(apt[...], gbuf[t, :, cols], NN))
        for peer in tensor_peers:
            value += qxr[peer, :, cols].astype(F32)
        value = value.astype(BF16)
        for k in range(shards):
            j = i * shards + k
            qsend[j] = value[:, k * qw : (k + 1) * qw]

            @pl.when(j != r)
            def _():
                q_copy(j).start()

        return carry

    def qg_copies():
        return [
            remote(qf.at[t, r], qf.at[t, r], at("qg_s", o), at("qg_r", r), dp=peer)
            for o, peer in enumerate(dp_peers)
        ]

    def forward(j):
        return [
            remote(qf.at[t, j], qf.at[t, j], at("qf_s", o * dp + j), at("qf_r", t * dp + j), tensor=peer)
            for o, peer in enumerate(tensor_peers)
        ]

    def reduce_q():
        from_dp(qrcv, "qp")
        total = qsend[r].astype(F32)
        for peer in dp_peers:
            total += qrcv[peer].astype(F32)
        qf[t, r] = (total * (1.0 / dp)).astype(BF16)
        start(qg_copies())
        start(forward(r))

    lax.fori_loop(0, third, q_unit, 0)

    from_tensor(gb, "gram")
    gram = gb[0]
    for tt in range(1, tensor):
        gram += gb[tt]
    inverse = inverse_factor(gram)
    head = inverse.astype(BF16)
    rest = inverse - head.astype(F32)
    middle = rest.astype(BF16)
    last = (rest - middle.astype(F32)).astype(BF16)
    lin[...] = jnp.concatenate([head, middle, last], axis=0)

    def applied(rows):
        parts = mm(lin[...], rows, NN)
        return parts[:rank] + (parts[rank : 2 * rank] + parts[2 * rank :])


    def late_unit(i, carry):
        land_unit(i, 0)
        return q_unit(i, carry)

    lax.fori_loop(third, units - 1, late_unit, 0)
    p = applied(praw[...])
    p_out[...] = p
    fact[...] = terms(p).T
    middle_unit = min(units - 1, second + 2)
    lax.fori_loop(second, middle_unit, matrix_unit, 0)

    @pl.when(r < dp - shards)
    def _():
        reduce_q()

    late_unit(units - 1, 0)
    later_unit = min(units, middle_unit + 2)
    lax.fori_loop(middle_unit, later_unit, matrix_unit, 0)

    @pl.when(r >= dp - shards)
    def _():
        reduce_q()

    lax.fori_loop(later_unit, units, matrix_unit, 0)

    def gather_q(j, carry):
        @pl.when(j != r)
        def _():
            remote(qf.at[t, j], qf.at[t, j], at("qg_s"), at("qg_r", j), dp=j).wait_recv()
            start(forward(j))

        return carry

    lax.fori_loop(0, dp, gather_q, 0)
    for j in range(dp):
        q_own[:, j * qw : (j + 1) * qw] = applied(qf[t, j])
    for peer in tensor_peers:
        for j in range(dp):
            remote(qf.at[peer, j], qf.at[peer, j], at("qf_s"), at("qf_r", peer * dp + j), tensor=peer).wait_recv()
    for tt in range(tensor):
        for j in range(dp):
            begin = tt * features + j * qw
            value = applied(qf[tt, j]).astype(BF16)
            pair[:rank, begin : begin + qw] = value
            pair[rank:, begin : begin + qw] = value

    @pl.when(section == 0)
    def _():
        q0_copy.wait_send()

    @pl.when(section == 1)
    def _():
        gx_copy.wait_send()
        for i in range(units):
            bulk_copy(i).wait_send()

    for copies in (q_copies, gq_copies, p_copies, pg_copies, gram_copies, ap_copies,
                   qx_copies, qg_copies()):
        sent(copies)

    def rows_sent(j, carry):
        sent(forward(j))

        @pl.when(j != r)
        def _():
            q_copy(j).wait_send()

        return carry

    lax.fori_loop(0, dp, rows_sent, 0)

    def g_sent(i, carry):
        sent(g_copies(i))
        return carry

    lax.fori_loop(0, units, g_sent, 0)


def chain(mesh, attn, gtop, branch, err, q_t):
    tensor, dp = mesh.shape["tensor"], mesh.shape["dp"]
    tokens, head_rows = attn.shape
    features = gtop.shape[1]
    rank = q_t.shape[0]
    tiles = max(1, head_rows // max(128, head_rows // 8))
    width = tensor * features
    pw, qw = head_rows // dp, features // dp
    units = features // max(128, features // 8, qw)
    names, count = semaphore_map(tensor, dp, units, tiles)
    wide = max(head_rows, features)
    vmem = pl.BlockSpec(memory_space=pltpu.VMEM)
    anywhere = pl.BlockSpec(memory_space=pl.ANY)
    args = [pltpu.with_memory_space_constraint(x, pltpu.HBM) for x in (attn, gtop, branch, err, q_t)]
    return pl.pallas_call(
        functools.partial(chain_kernel, (tensor, dp, units, tiles, names)),
        out_shape=(
            pltpu.VMEM((head_rows, width), BF16),
            pltpu.VMEM((tokens, features), BF16),
            pltpu.VMEM((rank, head_rows), F32),
            pltpu.VMEM((head_rows, 2 * rank), BF16),
            pltpu.VMEM((2 * rank, width), BF16),
            pltpu.VMEM((rank, features), F32),
        ),
        in_specs=[anywhere] * 5,
        out_specs=(vmem,) * 6,
        scratch_shapes=[
            pltpu.VMEM((tokens, head_rows), BF16),
            pltpu.VMEM((tokens, features), BF16),
            pltpu.VMEM((tokens, features), BF16),
            pltpu.VMEM((head_rows, width), BF16),
            pltpu.VMEM((rank, features), F32),
            pltpu.VMEM((head_rows, tokens), BF16),
            pltpu.VMEM((tensor, 2 * rank, features), BF16),
            pltpu.VMEM((rank, features), BF16),
            pltpu.VMEM((tensor, tokens, features), BF16),
            pltpu.VMEM((rank, tokens), BF16),
            pltpu.VMEM((rank, tokens), BF16),
            pltpu.VMEM((tensor, rank, tokens), F32),
            pltpu.VMEM((rank, wide), F32),
            pltpu.VMEM((dp, rank, pw), BF16),
            pltpu.VMEM((dp, rank, pw), BF16),
            pltpu.VMEM((dp, rank, pw), BF16),
            pltpu.VMEM((rank, head_rows), BF16),
            pltpu.VMEM((tensor, rank, rank), F32),
            pltpu.VMEM((3 * rank, rank), BF16),
            pltpu.VMEM((tensor, rank, tokens), F32),
            pltpu.VMEM((2 * rank, tokens), BF16),
            pltpu.VMEM((max(1, tensor - 1), rank, features), BF16),
            pltpu.VMEM((tensor, rank, features), BF16),
            pltpu.VMEM((dp, rank, qw), BF16),
            pltpu.VMEM((dp, rank, qw), BF16),
            pltpu.VMEM((tensor, dp, rank, qw), BF16),
            pltpu.SemaphoreType.DMA((count,)),
        ],
        compiler_params=pltpu.CompilerParams(
            collective_id=0, has_side_effects=True, vmem_limit_bytes=43 * 2**20
        ),
        name="chain",
    )(*args)


def finish_kernel(tiles, matrix, grad_in, p, fact, pair, q_own, out, grad_out, p_out, q_out, held, sem):
    head_rows, width = matrix.shape
    tile = head_rows // tiles
    step = min(width, 512)

    def out_copy(i):
        rows = pl.ds(pl.multiple_of(i * tile, tile), tile)
        return pltpu.make_async_copy(held.at[rows], out.at[rows], sem.at[i])

    def row_tile(i, carry):
        rows = pl.ds(pl.multiple_of(i * tile, tile), tile)
        for c in range(width // step):
            here = slice(c * step, (c + 1) * step)
            value = matrix[rows, here].astype(F32) - mm(fact[rows, :], pair[:, here], NN)
            held[rows, here] = value.astype(BF16)
        out_copy(i).start()
        return carry

    small = [
        pltpu.make_async_copy(src, dst, sem.at[tiles + i])
        for i, (src, dst) in enumerate(((grad_in, grad_out), (p, p_out), (q_own, q_out)))
    ]
    for copy in small:
        copy.start()
    lax.fori_loop(0, tiles, row_tile, 0)
    for copy in small:
        copy.wait()

    def landed(i, carry):
        out_copy(i).wait()
        return carry

    lax.fori_loop(0, tiles, landed, 0)


def finish(matrix, grad_in, p, fact, pair, q_own):
    head_rows, width = matrix.shape
    tiles = max(1, head_rows // max(128, head_rows // 16))
    vmem = pl.BlockSpec(memory_space=pltpu.VMEM)
    anywhere = pl.BlockSpec(memory_space=pl.ANY)
    args = [
        pltpu.with_memory_space_constraint(x, pltpu.VMEM)
        for x in (matrix, grad_in, p, fact, pair, q_own)
    ]
    return pl.pallas_call(
        functools.partial(finish_kernel, tiles),
        out_shape=(
            pltpu.HBM(matrix.shape, BF16),
            pltpu.HBM(grad_in.shape, BF16),
            pltpu.HBM(p.shape, F32),
            pltpu.HBM(q_own.shape, F32),
        ),
        in_specs=[vmem] * 6,
        out_specs=(anywhere,) * 4,
        scratch_shapes=[
            pltpu.VMEM((head_rows, width), BF16),
            pltpu.SemaphoreType.DMA((tiles + 3,)),
        ],
        compiler_params=pltpu.CompilerParams(vmem_limit_bytes=20 * 2**20),
        name="finish",
    )(*args)


def on_device(mesh, attn_out, grad_top, branch_grad, error_prev, q_prev):
    micro, rows, features = grad_top.shape
    tokens = micro * rows
    attn = attn_out.reshape(tokens, attn_out.shape[3])
    gtop = grad_top.reshape(tokens, features)
    branch = branch_grad.reshape(tokens, features)
    err = error_prev[0, 0]
    error, grad_in, p, q_own = finish(*chain(mesh, attn, gtop, branch, err, q_prev[0].T))
    return grad_in.reshape(branch_grad.shape), error[None, None], p.T[None], q_own.T[None]


def solution(mesh):
    assert mesh.shape["pipe"] == 2
    return jax.shard_map(
        functools.partial(on_device, mesh),
        mesh=mesh,
        in_specs=(
            P("pipe", None, "dp", "tensor"),
            P(None, "dp", "tensor"),
            P("pipe", None, "dp", "tensor"),
            P("pipe", "dp", "tensor", None),
            P("pipe", "tensor", None),
        ),
        out_specs=(
            P("pipe", None, "dp", "tensor"),
            P("pipe", "dp", "tensor", None),
            P("pipe", "tensor", None),
            P("pipe", "tensor", None),
        ),
        check_vma=False,
    )
```

profile of v0, /device:TPU:1, one launch (start us, length us, event | category | flops | bytes accessed | tf_op | source)
XLA Modules:
  0.0 77.8 jit_solution(2638538672867742693)
XLA Ops:
  0.6 69.2 %chain.1 = (bf16[2048,4096]{1,0:T(8,128)(2,1)S(1)}, bf16[512,2048]{1,0:T(8,128)(2,1)S(1)}, f32[64,2048]{1,0:T(8,128)S(1)}, bf16[2048,128]{1,0:T(8,128)(2,1)S(1)}...) custom-call(bf16[512,2048]{1,0:T(8,128)(2,1)} %bitcast.16, bf16[512,2048]{1,0:T(8,128)(2,1)} %bitcast.17, ...), custom_call_target="tpu_custom_call" | custom-call | tf_op jit(solution)/shard_map/chain/pallas_call | solution.py:478
  69.8 8.0 %finish.1 = (bf16[2048,4096]{1,0:T(8,128)(2,1)}, bf16[512,2048]{1,0:T(8,128)(2,1)}, f32[64,2048]{1,0:T(8,128)}, f32[64,2048]{1,0:T(8,128)}) custom-call(bf16[2048,4096]{1,0:T(8,128)(2,1)S(1)} %get-tuple-element.14.matrix, bf16[512,2048]{1,0:T(8,128)(2,1)S(1)} %get-tuple-element.15.grad_in, f32[64,2048]{1,0:T(8,128)S(1)} %get-tuple-element.16.p, ...), custom_call_target="tpu_custom_call" | custom-call | tf_op jit(solution)/shard_map/finish/pallas_call | solution.py:570
where the time goes:
time: 78 us; the launch traced here: 77.8 us
  Pallas kernels  77.2 us (99%)
    pallas_call x1, Pallas kernels, chain(): pl.pallas_call(functools.partial(chain_kernel, (tensor, dp, units, tiles,...  69.2 us
    pallas_call x1, Pallas kernels, finish(): pl.pallas_call(functools.partial(finish_kernel, tiles), out_shape=(pltpu....  7.96 us

commit v1 on v0

--- a/solution.py
+++ b/solution.py
@@ -130,6 +130,11 @@
         for copy in copies:
             copy.wait_send()
 
+    late = units // 2
+
+    def place(i):
+        return (i + late + 1) % units
+
     def columns(i):
         return pl.ds(pl.multiple_of(i * unit, unit), unit)
 
@@ -174,7 +179,7 @@
     @pl.when(section == 1)
     def _():
         for i in range(ahead):
-            bulk_copy(i).start()
+            bulk_copy(place(i)).start()
 
     q_copies = over_tensor(qg.at[t], qg, "q")
     start(q_copies)
@@ -205,7 +210,7 @@
         gqx[...] = (mm(q0[...], grad_in[...], NT) * scale).astype(BF16)
         gx_copy.start()
         for i in range(ahead, units):
-            bulk_copy(i).start()
+            bulk_copy(place(i)).start()
 
     @pl.when(section == 0)
     def _():
@@ -232,6 +237,7 @@
         ]
 
     def land_unit(i, carry):
+        i = place(i)
         cols = columns(i)
 
         @pl.when(section == 0)
@@ -249,6 +255,7 @@
         return carry
 
     def matrix_unit(i, carry):
+        i = place(i)
         cols = columns(i)
         for peer in tensor_peers:
             here = gbuf.at[peer, :, cols]
@@ -329,6 +336,7 @@
         return remote(qsend.at[j], qrcv.at[r], at("qp_s", j), at("qp_r", r), dp=j)
 
     def q_unit(i, carry):
+        i = place(i)
         cols = columns(i)
         value = eq[:, cols] + fold(mm(apt[...], gbuf[t, :, cols], NN))
         for peer in tensor_peers:
@@ -394,7 +402,7 @@
     middle_unit = min(units - 1, second + 2)
     lax.fori_loop(second, middle_unit, matrix_unit, 0)
 
-    @pl.when(r < dp - shards)
+    @pl.when(r // shards != late)
     def _():
         reduce_q()
 
@@ -402,32 +410,34 @@
     later_unit = min(units, middle_unit + 2)
     lax.fori_loop(middle_unit, later_unit, matrix_unit, 0)
 
-    @pl.when(r >= dp - shards)
+    @pl.when(r // shards == late)
     def _():
         reduce_q()
 
+    order = [(j + (late + 1) * shards) % dp for j in range(dp)]
+
+    def gather_q(owners):
+        for j in owners:
+            @pl.when(r != j)
+            def _(j=j):
+                remote(qf.at[t, j], qf.at[t, j], at("qg_s"), at("qg_r", j), dp=j).wait_recv()
+                start(forward(j))
+
+        for j in owners:
+            q_own[:, j * qw : (j + 1) * qw] = applied(qf[t, j])
+        for peer in tensor_peers:
+            for j in owners:
+                remote(qf.at[peer, j], qf.at[peer, j], at("qf_s"), at("qf_r", peer * dp + j), tensor=peer).wait_recv()
+        for tt in range(tensor):
+            for j in owners:
+                begin = tt * features + j * qw
+                value = applied(qf[tt, j]).astype(BF16)
+                pair[:rank, begin : begin + qw] = value
+                pair[rank:, begin : begin + qw] = value
+
+    gather_q(order[: dp - shards])
     lax.fori_loop(later_unit, units, matrix_unit, 0)
-
-    def gather_q(j, carry):
-        @pl.when(j != r)
-        def _():
-            remote(qf.at[t, j], qf.at[t, j], at("qg_s"), at("qg_r", j), dp=j).wait_recv()
-            start(forward(j))
-
-        return carry
-
-    lax.fori_loop(0, dp, gather_q, 0)
-    for j in range(dp):
-        q_own[:, j * qw : (j + 1) * qw] = applied(qf[t, j])
-    for peer in tensor_peers:
-        for j in range(dp):
-            remote(qf.at[peer, j], qf.at[peer, j], at("qf_s"), at("qf_r", peer * dp + j), tensor=peer).wait_recv()
-    for tt in range(tensor):
-        for j in range(dp):
-            begin = tt * features + j * qw
-            value = applied(qf[tt, j]).astype(BF16)
-            pair[:rank, begin : begin + qw] = value
-            pair[rank:, begin : begin + qw] = value
+    gather_q(order[dp - shards :])
 
     @pl.when(section == 0)
     def _():

time: 78 us -> 76.4 us (0.979)
  Pallas kernels: 77.2 us -> 75.6 us
    pallas_call x1, Pallas kernels: 69.2 us -> 67.6 us  [chain(): pl.pallas_call(functools.partial(chain_kernel, (tensor, dp, units, tiles,...]
where the time goes in v1:
time: 76.4 us; the launch traced here: 76.2 us
  Pallas kernels  75.6 us (99%)
    pallas_call x1, Pallas kernels, chain(): pl.pallas_call(functools.partial(chain_kernel, (tensor, dp, units, tiles,...  67.6 us
    pallas_call x1, Pallas kernels, finish(): pl.pallas_call(functools.partial(finish_kernel, tiles), out_shape=(pltpu....  7.95 us

profile of v1, /device:TPU:1, one launch (start us, length us, event | category | flops | bytes accessed | tf_op | source)
XLA Modules:
  0.0 76.2 jit_solution(5091608305070726683)
XLA Ops:
  0.6 67.6 %chain.1 = (bf16[2048,4096]{1,0:T(8,128)(2,1)S(1)}, bf16[512,2048]{1,0:T(8,128)(2,1)S(1)}, f32[64,2048]{1,0:T(8,128)S(1)}, bf16[2048,128]{1,0:T(8,128)(2,1)S(1)}...) custom-call(bf16[512,2048]{1,0:T(8,128)(2,1)} %bitcast.16, bf16[512,2048]{1,0:T(8,128)(2,1)} %bitcast.17, ...), custom_call_target="tpu_custom_call" | custom-call | tf_op jit(solution)/shard_map/chain/pallas_call | solution.py:488
  68.2 7.9 %finish.1 = (bf16[2048,4096]{1,0:T(8,128)(2,1)}, bf16[512,2048]{1,0:T(8,128)(2,1)}, f32[64,2048]{1,0:T(8,128)}, f32[64,2048]{1,0:T(8,128)}) custom-call(bf16[2048,4096]{1,0:T(8,128)(2,1)S(1)} %get-tuple-element.14.matrix, bf16[512,2048]{1,0:T(8,128)(2,1)S(1)} %get-tuple-element.15.grad_in, f32[64,2048]{1,0:T(8,128)S(1)} %get-tuple-element.16.p, ...), custom_call_target="tpu_custom_call" | custom-call | tf_op jit(solution)/shard_map/finish/pallas_call | solution.py:580
